TPU v7x, 32 devices: a whole 2x2x4 slice. The times are simulated.
32 devices in a mesh: nest: 4 (over y, x), tile: 8 (over z, core).
Axes of the slice: x: 2, y: 2, z: 4, core: 2. Of those that a mesh axis runs over, the one named last changes fastest.
Arguments:
- child_fields: float32 [4, 32, 192, 384], P('nest', None, 'tile'), may hold values from -18 to 18
- row_weights: float32 [8, 24], replicated
- col_weights: float32 [384, 128], replicated
- nest_offsets: int32 [4, 2], replicated, may hold values from 0 to 960, as said below
- priority: int32 [128, 1024], P('tile', 'nest'), may hold values from -1 to 3, as said below
- parent_old: float32 [32, 128, 1024], P(None, 'tile', 'nest'), may hold values from -6 to 6
- smooth_rate: float32 [32], replicated, may hold values from 0.03 to 0.22
Outputs:
- parent_new: float32 [32, 128, 1024], P(None, 'tile', 'nest')
Inputs may be any that keep to these rules, and one draw needn't show every extreme that they name: nest_offsets[n, 0] lies in 0 .. 960 and nest_offsets[n, 1] in 0 .. 127. priority[x, y] is -1 or a nest n with nest_offsets[n, 0] <= y < nest_offsets[n, 0] + 64.
All inputs are finite; a program needn't handle non-finite values.
Results may differ from a plain program's by a relative error of at most 0.000058.
Values sent between devices are 32-bit elements; how exact they have to be, the bound alone decides.
A program may use at most 128 MiB of HBM per device.

v0:
```python
import jax
import jax.numpy as jnp
from jax import lax
from jax.sharding import PartitionSpec as P


def with_halo(value, sides, width):
    for axis, dim in sides:
        count, length = (lax.axis_size(axis), value.shape[dim])
        up = [(i, (i + 1) % count) for i in range(count)]
        down = [(j, i) for i, j in up]
        last = lax.slice_in_dim(value, length - width, length, axis=dim)
        leading = lax.slice_in_dim(value, 0, width, axis=dim)
        before = lax.ppermute(last, axis, up)
        after = lax.ppermute(leading, axis, down)
        value = jnp.concatenate([before, value, after], axis=dim)
    return value


def place_slabs(
    merged_now, slabs, first_nest, nest_offsets, priority, own_start, owned_rows, nrows
):
    planes = merged_now.shape[0]
    strip_cols = merged_now.shape[1]
    for member in range(slabs.shape[0]):
        nest_num = first_nest + member
        local_top = nest_offsets[nest_num, 0] - own_start
        position = jnp.clip(local_top + nrows, 0, owned_rows + nrows)
        framed = jnp.zeros((planes, strip_cols, owned_rows + 2 * nrows), jnp.float32)
        framed = lax.dynamic_update_slice(
            framed, slabs[member], (jnp.int32(0), jnp.int32(0), position)
        )
        window = framed[:, :, nrows : nrows + owned_rows]
        merged_now = jnp.where((priority == nest_num)[None], window, merged_now)
    return merged_now


def per_device(
    child_fields, row_weights, col_weights, nest_offsets, priority, parent_old, smooth_rate
):
    child_block = child_fields[0]
    planes = child_block.shape[0]
    cell_rows = row_weights.shape[0]
    tile_count = lax.axis_size("tile")
    nest_count = lax.axis_size("nest")
    strip_cols = parent_old.shape[1]
    owned_rows = parent_old.shape[2]
    nrows = cell_rows * tile_count
    nest_id = lax.axis_index("nest")
    own_start = nest_id * owned_rows
    thinned = jnp.einsum("pr,frc->fpc", row_weights, child_block, precision=lax.Precision.HIGHEST)
    restricted = jnp.einsum("fpc,cx->xfp", thinned, col_weights, precision=lax.Precision.HIGHEST)
    rolled = jnp.roll(restricted, nest_offsets[nest_id, 1], axis=0)
    outgoing = rolled.reshape(rolled.shape[0], planes * cell_rows)
    arrived = lax.all_to_all(outgoing, "tile", split_axis=0, concat_axis=0, tiled=True)
    column_slab = arrived.reshape(tile_count, strip_cols, planes, cell_rows)
    column_slab = column_slab.transpose(2, 1, 0, 3).reshape(planes, strip_cols, nrows)
    merged = place_slabs(
        parent_old,
        lax.all_gather(column_slab[None], "nest", axis=0, tiled=True),
        jnp.int32(0),
        nest_offsets,
        priority,
        own_start,
        owned_rows,
        nrows,
    )
    padded = with_halo(merged, (("nest", 2), ("tile", 1)), 1)
    west_side = padded[:, :-2, 1:-1]
    east_side = padded[:, 2:, 1:-1]
    south_side = padded[:, 1:-1, :-2]
    north_side = padded[:, 1:-1, 2:]
    south_side = jnp.where(
        nest_id == 0, jnp.concatenate([merged[:, :, :1], south_side[:, :, 1:]], axis=2), south_side
    )
    north_side = jnp.where(
        nest_id == nest_count - 1,
        jnp.concatenate([north_side[:, :, :-1], merged[:, :, -1:]], axis=2),
        north_side,
    )
    return merged + smooth_rate[:, None, None] * (
        east_side + west_side + north_side + south_side - 4.0 * merged
    )


def solution(mesh):
    return jax.shard_map(
        per_device,
        mesh=mesh,
        in_specs=(
            P("nest", None, "tile", None),
            P(),
            P(),
            P(),
            P("tile", "nest"),
            P(None, "tile", "nest"),
            P(),
        ),
        out_specs=P(None, "tile", "nest"),
        check_vma=False,
    )
```

profile of v0, /device:TPU:0, one launch (start us, length us, event | category | flops | bytes accessed | tf_op | source)
XLA Modules:
  0.0 76.2 jit_solution(5162463367798320528)
XLA Ops:
  0.0 1.5 %fusion.17 = (s32[1,1]{0,1:T(1,128)}, s32[1,1]{0,1:T(1,128)}, s32[1,1]{0,1:T(1,128)}, s32[1,1]{0,1:T(1,128)}, s32[1,1]{0,1:T(1,128)}) fusion(s32[4,2]{0,1:T(2,128)} %param.10, s32[]{:T(128)S(6)} %select_n.47), kind=kLoop, calls=%fused_computation.42 | loop fusion | bytes 44 | tf_op jit(solution)/shard_map/dynamic_slice | solution.py:27
  3.5 1.5 %convolution_bitcast_fusion = f32[32,8,384]{2,1,0:T(8,128)S(1)} fusion(f32[1,32,24,384]{3,2,1,0:T(8,128)S(1)} %copy-done, f32[8,24]{1,0:T(8,128)} %param.8), kind=kOutput, calls=%fused_computation | convolution fusion | flops 28311552 | bytes 1573632 | tf_op jit(solution)/shard_map/pr,frc->fpc/dot_general | solution.py:51
  5.0 0.5 convolution_bitcast_fusion.1
  5.6 0.3 all_to_all.6
  5.9 1.0 %copy.14 = f32[8,16,256]{2,1,0:T(8,128)} copy(f32[8,16,256]{1,0,2:T(8,128)S(1)} %all_to_all.6) | data formatting | bytes 262144 | tf_op jit(solution)/shard_map/all_to_all | solution.py:55
  7.0 6.4 %all-to-all-start = ((f32[8,16,256]{2,1,0:T(8,128)}), f32[8,16,256]{2,1,0:T(8,128)S(1)}, u32[]{:S(2)}, u32[]{:S(2)}) async-start(f32[8,16,256]{2,1,0:T(8,128)} %copy.14), calls=%async_computation | async-start | bytes 262144 | tf_op jit(solution)/shard_map/all_to_all | solution.py:55
  15.9 4.1 %all-to-all-done = f32[8,16,256]{2,1,0:T(8,128)S(1)} async-done(((f32[8,16,256]{2,1,0:T(8,128)}), f32[8,16,256]{2,1,0:T(8,128)S(1)}, u32[]{:S(2)}, u32[]{:S(2)}) %all-to-all-start) | async-done | bytes 131104 | tf_op jit(solution)/shard_map/all_to_all | solution.py:55
  20.1 0.3 copy.15
  20.4 0.6 copy.16
  21.0 0.2 copy.17
  21.2 12.9 %all_gather.3 = f32[4,32,16,64]{3,2,1,0:T(8,128)S(1)} all-gather(f32[1,32,16,64]{3,2,1,0:T(8,128)S(1)} %copy.17), channel_id=1, replica_groups=mesh['nest'=4,'tile'=8] {'nest'}, dimensions={0}, use_global_device_ids=true | all-gather | bytes 655360 | tf_op jit(solution)/shard_map/all_gather | solution.py:60
  34.3 4.8 %dynamic_update_slice.12 = f32[32,16,384]{2,1,0:T(8,128)S(1)} dynamic-update-slice(f32[32,16,384]{2,1,0:T(8,128)S(1)} %broadcast.9.clone.3, f32[32,16,64]{2,1,0:T(8,128)S(1)} %get-tuple-element.7, s32[]{:T(128)} %constant.44.clone.1, s32[]{:T(128)} %constant.44.clone.1, s32[]{:T(128)S(6)} %min.13) | dynamic-update-slice | bytes 262148 | tf_op jit(solution)/shard_map/dynamic_update_slice | solution.py:30
  39.2 4.8 %dynamic_update_slice.13 = f32[32,16,384]{2,1,0:T(8,128)S(1)} dynamic-update-slice(f32[32,16,384]{2,1,0:T(8,128)S(1)} %broadcast.9.clone.2, f32[32,16,64]{2,1,0:T(8,128)S(1)} %get-tuple-element.10, s32[]{:T(128)} %constant.44.clone.1, s32[]{:T(128)} %constant.44.clone.1, s32[]{:T(128)S(6)} %min.14) | dynamic-update-slice | bytes 262148 | tf_op jit(solution)/shard_map/dynamic_update_slice | solution.py:30
  44.0 1.0 %broadcast.9.clone.1 = f32[32,16,384]{2,1,0:T(8,128)} broadcast(f32[]{:T(128)} %constant.20.clone.1), dimensions={} | broadcast | bytes 786436 | tf_op jit(solution)/shard_map/broadcast.1
  45.1 6.3 %dynamic_update_slice.14 = f32[32,16,384]{2,1,0:T(8,128)} dynamic-update-slice(f32[32,16,384]{2,1,0:T(8,128)} %broadcast.9.clone.1, f32[32,16,64]{2,1,0:T(8,128)S(1)} %get-tuple-element.9, s32[]{:T(128)} %constant.44.clone.1, s32[]{:T(128)} %constant.44.clone.1, s32[]{:T(128)S(6)} %min.15) | dynamic-update-slice | bytes 262148 | tf_op jit(solution)/shard_map/dynamic_update_slice | solution.py:30
  51.4 4.9 %dynamic_update_slice.15 = f32[32,16,384]{2,1,0:T(8,128)S(1)} dynamic-update-slice(f32[32,16,384]{2,1,0:T(8,128)S(1)} %broadcast.9.clone, f32[32,16,64]{2,1,0:T(8,128)S(1)} %get-tuple-element.8, s32[]{:T(128)} %constant.44.clone.1, s32[]{:T(128)} %constant.44.clone.1, s32[]{:T(128)S(6)} %min.16) | dynamic-update-slice | bytes 262148 | tf_op jit(solution)/shard_map/dynamic_update_slice | solution.py:30
  56.3 2.1 %fusion.11 = f32[32,16,256]{2,1,0:T(8,128)S(1)} fusion(f32[32,16,256]{2,1,0:T(8,128)} %param.12, f32[32,16,384]{2,1,0:T(8,128)S(1)} %dynamic_update_slice.15, f32[32,16,384]{2,1,0:T(8,128)} %dynamic_update_slice.14, f32[32,16,384]{2,1,0:T(8,128)} %copy-done.1, f32[32,16,384]{2,1,0:T(8,128)S(1)} %dynamic_update_slice.12, ...), kind=kLoop, calls=%fused_computation.22 | loop fusion | flops 524288 | bytes 3162112 | tf_op jit(solution)/shard_map/jit(_where)/select_n | solution.py:34
  58.7 2.9 %collective-permute-start.1 = (f32[32,16,1]{2,1,0:T(8,128)S(1)}, f32[32,16,1]{2,1,0:T(8,128)S(1)}, u32[]{:S(2)}, u32[]{:S(2)}) collective-permute-start(f32[32,16,1]{2,1,0:T(8,128)S(1)} %get-tuple-element.13), channel_id=1, source_target_pairs={{8,0},{16,8},{24,16},{0,24},{9,1},{17,9},{25,17},{1,25},{10,2},{18... | collective-permute-start | bytes 6152 | tf_op jit(solution)/shard_map/ppermute | solution.py:15
  61.6 7.0 %collective-permute-done = f32[32,16,1]{2,1,0:T(8,128)S(1)} collective-permute-done((f32[32,16,1]{2,1,0:T(8,128)S(1)}, f32[32,16,1]{2,1,0:T(8,128)S(1)}, u32[]{:S(2)}, u32[]{:S(2)}) %collective-permute-start) | collective-permute-done | bytes 2080 | tf_op jit(solution)/shard_map/ppermute | solution.py:14
  68.6 0.3 pad_maximum_fusion.10
  69.0 0.5 collective-permute-start.3
  69.7 1.0 %collective-permute-done.2 = f32[32,1,258]{2,1,0:T(1,128)S(1)} collective-permute-done((f32[32,1,258]{2,1,0:T(1,128)S(1)}, f32[32,1,258]{2,1,0:T(1,128)S(1)}, u32[]{:S(2)}, u32[]{:S(2)}) %collective-permute-start.2) | collective-permute-done | bytes 33056 | tf_op jit(solution)/shard_map/ppermute | solution.py:15
  70.8 3.6 %collective-permute-done.3 = f32[32,1,258]{2,1,0:T(1,128)S(1)} collective-permute-done((f32[32,1,258]{2,1,0:T(1,128)S(1)}, f32[32,1,258]{2,1,0:T(1,128)S(1)}, u32[]{:S(2)}, u32[]{:S(2)}) %collective-permute-start.3) | collective-permute-done | bytes 33056 | tf_op jit(solution)/shard_map/ppermute | solution.py:14
  74.4 1.8 %fusion.5 = f32[32,16,256]{2,1,0:T(8,128)} fusion(f32[32,16,256]{2,1,0:T(8,128)S(1)} %fusion.11, f32[32,16,1]{2,1,0:T(8,128)S(1)} %collective-permute-done, f32[32,16,1]{2,1,0:T(8,128)S(1)} %collective-permute-done.1, f32[32,1,258]{2,1,0:T(1,128)S(1)} %collective-permute-done.3, f32[32,1,258]{2,1,0:T(1,128)S(1)} %collective-permute-done.2, ...), kind=kLoop, calls=%fused_computation.8 | loop fusion | flops 2490368 | bytes 2167426 | tf_op jit(solution)/shard_map/add | solution.py:81
  (21 shorter events, 0.9 us)
Async XLA Ops:
  0.0 3.5 %copy-start = (f32[1,32,24,384]{3,2,1,0:T(8,128)S(1)}, f32[1,32,24,384]{3,2,1,0:T(8,128)}, u32[]{:S(2)}) copy-start(f32[1,32,24,384]{3,2,1,0:T(8,128)} %param.7) | copy-start | bytes 3538948
  0.0 5.0 %copy-start.2 = (f32[384,128]{1,0:T(8,128)S(1)}, f32[384,128]{1,0:T(8,128)}, u32[]{:S(2)}) copy-start(f32[384,128]{1,0:T(8,128)} %param.9) | copy-start | bytes 589828
  5.6 10.3 %copy-start.3 = (s32[16,256]{1,0:T(8,128)S(1)}, s32[16,256]{1,0:T(8,128)}, u32[]{:S(2)}) copy-start(s32[16,256]{1,0:T(8,128)} %param.11) | copy-start | bytes 49156
  7.0 13.1 %all-to-all-start = ((f32[8,16,256]{2,1,0:T(8,128)}), f32[8,16,256]{2,1,0:T(8,128)S(1)}, u32[]{:S(2)}, u32[]{:S(2)}) async-start(f32[8,16,256]{2,1,0:T(8,128)} %copy.14), calls=%async_computation | async-start | bytes 262144 | tf_op jit(solution)/shard_map/all_to_all | solution.py:55
  44.0 7.4 %copy-start.1 = (f32[32,16,384]{2,1,0:T(8,128)}, f32[32,16,384]{2,1,0:T(8,128)S(1)}, u32[]{:S(2)}) copy-start(f32[32,16,384]{2,1,0:T(8,128)S(1)} %dynamic_update_slice.13) | copy-start | bytes 2359300
  58.6 10.0 %collective-permute-start = (f32[32,16,1]{2,1,0:T(8,128)S(1)}, f32[32,16,1]{2,1,0:T(8,128)S(1)}, u32[]{:S(2)}, u32[]{:S(2)}) collective-permute-start(f32[32,16,1]{2,1,0:T(8,128)S(1)} %get-tuple-element.14), channel_id=1, source_target_pairs={{0,8},{8,16},{16,24},{24,0},{1,9},{9,17},{17,25},{25,1},{2,10},{10... | collective-permute-start | bytes 6152 | tf_op jit(solution)/shard_map/ppermute | solution.py:14
  58.7 9.9 %collective-permute-start.1 = (f32[32,16,1]{2,1,0:T(8,128)S(1)}, f32[32,16,1]{2,1,0:T(8,128)S(1)}, u32[]{:S(2)}, u32[]{:S(2)}) collective-permute-start(f32[32,16,1]{2,1,0:T(8,128)S(1)} %get-tuple-element.13), channel_id=1, source_target_pairs={{8,0},{16,8},{24,16},{0,24},{9,1},{17,9},{25,17},{1,25},{10,2},{18... | collective-permute-start | bytes 6152 | tf_op jit(solution)/shard_map/ppermute | solution.py:15
  69.0 5.4 %copy-start.4 = (f32[32]{0:T(128)S(1)}, f32[32]{0:T(128)}, u32[]{:S(2)}) copy-start(f32[32]{0:T(128)} %param.13) | copy-start | bytes 388
  69.0 1.8 %collective-permute-start.2 = (f32[32,1,258]{2,1,0:T(1,128)S(1)}, f32[32,1,258]{2,1,0:T(1,128)S(1)}, u32[]{:S(2)}, u32[]{:S(2)}) collective-permute-start(f32[32,1,258]{2,1,0:T(1,128)S(1)} %get-tuple-element.5), channel_id=1, source_target_pairs={{1,0},{2,1},{3,2},{4,3},{5,4},{6,5},{7,6},{0,7},{9,8},{10,9},{11,1... | collective-permute-start | bytes 99080 | tf_op jit(solution)/shard_map/ppermute | solution.py:15
  69.0 5.4 %collective-permute-start.3 = (f32[32,1,258]{2,1,0:T(1,128)S(1)}, f32[32,1,258]{2,1,0:T(1,128)S(1)}, u32[]{:S(2)}, u32[]{:S(2)}) collective-permute-start(f32[32,1,258]{2,1,0:T(1,128)S(1)} %get-tuple-element.6), channel_id=1, source_target_pairs={{0,1},{1,2},{2,3},{3,4},{4,5},{5,6},{6,7},{7,0},{8,9},{9,10},{10,1... | collective-permute-start | bytes 99080 | tf_op jit(solution)/shard_map/ppermute | solution.py:14
where the time goes:
time: 77 us; the launch traced here: 76.2 us
  local copies, waits for them, and re-layouts  26.5 us (34%)
  waiting for transfers between devices  15.8 us (21%)
  blocking collectives  12.9 us (17%)
  starting transfers between devices  9.88 us (13%)
  between operations  4.73 us (6%)
  other arithmetic  4.38 us (6%)
  matrix products  1.93 us (3%)
    dynamic_update_slice x4, local copies, waits for them, and re-layouts, place_slabs(): lax.dynamic_update_slice(framed, slabs[member], (jnp.int32(0), jnp.int32(...  20.9 us
    all_gather x1, blocking collectives, per_device(): lax.all_gather(column_slab[None], 'nest', axis=0, tiled=True)  12.9 us
    ppermute x2, waiting for transfers between devices, with_halo(): before = lax.ppermute(last, axis, up)  10.7 us
    all_to_all x1, starting transfers between devices, per_device(): lax.all_to_all(outgoing, 'tile', split_axis=0, concat_axis=0, tiled=True)  6.35 us
    all_to_all x1, waiting for transfers between devices, per_device(): lax.all_to_all(outgoing, 'tile', split_axis=0, concat_axis=0, tiled=True)  4.14 us
    ppermute x2, starting transfers between devices, with_halo(): after = lax.ppermute(leading, axis, down)  2.97 us
    select_n x1, other arithmetic, place_slabs(): merged_now = jnp.where((priority == nest_num)[None], window, merged_now)  2.14 us
    add x1, other arithmetic, per_device(): merged + smooth_rate[:, None, None] * (east_side + west_side + north_side...  1.75 us
  transfers between devices with their start and end apart: 5, of which 4 were waited for; matrix products, arithmetic and copies ran while one was open for 0% of the time, Pallas kernels for 0%

commit v1 on v0

v1 whole, which is shorter than its diff:
```python
import functools

import jax
import jax.numpy as jnp
from jax import lax
from jax.experimental import pallas as pl
from jax.experimental.pallas import tpu as pltpu
from jax.sharding import PartitionSpec as P

MESH = pl.DeviceIdType.MESH
LANES = 128
F32 = jnp.float32
BF16 = jnp.bfloat16


def split(value):
    high = value.astype(BF16)
    return high, (value - high.astype(F32)).astype(BF16)


def dot(a, b):
    return jnp.dot(a, b, preferred_element_type=F32)


def dot3(a, b):
    (ah, al), (bh, bl) = a, b
    return dot(ah, bh) + (dot(ah, bl) + dot(al, bh))


def remote(src, dst, send_sem, recv_sem, where):
    return pltpu.make_async_remote_copy(
        src_ref=src,
        dst_ref=dst,
        send_sem=send_sem,
        recv_sem=recv_sem,
        device_id=where,
        device_id_type=MESH,
    )


def kernel(
    tiles,
    nests,
    offs_ref,
    rate_ref,
    rw_ref,
    prio_ref,
    child_hbm,
    cw_hbm,
    parent_hbm,
    out_hbm,
    child,
    cw,
    merged,
    pieces,
    strips,
    ew_out,
    ew_in,
    ns_out,
    ns_in,
    result,
    child_sem,
    cw_sem,
    parent_sem,
    out_sem,
    a2a_send,
    a2a_recv,
    slab_send,
    slab_recv,
    edge_send,
    edge_recv,
):
    planes, crow, _ = child.shape
    prd = rw_ref.shape[0]
    cols, rows = prio_ref.shape
    per = LANES // cols
    groups = planes // per
    nrows = prd * tiles
    me_n, me_t = lax.axis_index("nest"), lax.axis_index("tile")

    def group(ref, g):
        return ref.at[pl.ds(g * per, per)]

    child_in = [
        pltpu.make_async_copy(group(child_hbm.at[0], g), group(child, g), child_sem.at[g])
        for g in range(groups)
    ]
    cw_in = pltpu.make_async_copy(cw_hbm, cw, cw_sem)
    parent_in = pltpu.make_async_copy(parent_hbm, merged, parent_sem)
    child_in[0].start()
    cw_in.start()
    for g in range(1, groups):
        child_in[g].start()
    parent_in.start()

    barrier = pltpu.get_barrier_semaphore()
    for d in range(1, tiles):
        pl.semaphore_signal(
            barrier, inc=1, device_id={"tile": lax.rem(me_t + d, tiles)}, device_id_type=MESH
        )
    for d in range(1, nests):
        pl.semaphore_signal(
            barrier, inc=1, device_id={"nest": lax.rem(me_n + d, nests)}, device_id_type=MESH
        )

    rw = rw_ref[...]
    spread_rows = lax.broadcasted_iota(jnp.int32, (per * crow, crow), 0)
    spread_cols = lax.broadcasted_iota(jnp.int32, (per * crow, crow), 1)
    spread = jnp.where(lax.rem(spread_rows, crow) == spread_cols, 1.0, 0.0).astype(BF16)
    wide_r = lax.broadcasted_iota(jnp.int32, (per * prd, per * crow), 0)
    wide_c = lax.broadcasted_iota(jnp.int32, (per * prd, per * crow), 1)
    diagonal = wide_r // prd == wide_c // crow
    block_rw = []
    for part in split(rw):
        line = lax.dot_general(
            part, spread, (((1,), (1,)), ((), ())), preferred_element_type=F32
        )
        line = jnp.concatenate([line] * per, axis=0)
        block_rw.append(jnp.where(diagonal, line, 0.0).astype(BF16))

    lane_group = lax.broadcasted_iota(jnp.int32, (prd, LANES), 1) // cols
    left = jnp.int32(0)
    for n in range(nests):
        left = jnp.where(me_n == n, offs_ref[n, 1], left)

    a2a = []
    cw_split = None
    for g in range(groups):
        child_in[g].wait()
        block = child[g * per : (g + 1) * per].reshape(per * crow, child.shape[2])
        thinned = dot3(block_rw, split(block))
        if g == 0:
            cw_in.wait()
            cw_split = split(cw[...])
        restricted = dot3(split(thinned), cw_split)
        restricted = pltpu.roll(restricted, left, 1)
        for t in range(tiles):
            base, off = (t * cols) // LANES * LANES, (t * cols) % LANES
            piece = None
            for j in range(per):
                part = restricted[j * prd : (j + 1) * prd, base : base + LANES]
                shift = (j * cols - off) % LANES
                if shift:
                    part = pltpu.roll(part, shift, 1)
                piece = part if j == 0 else jnp.where(lane_group == j, part, piece)
            pieces[g, t] = piece
        here = pl.ds(pl.multiple_of(me_t * prd, prd), prd)
        strips[me_n, g, here, :] = pieces[g, me_t]
        if g == 0:
            pl.semaphore_wait(barrier, tiles + nests - 2)
        for d in range(1, tiles):
            t = lax.rem(me_t + d, tiles)
            copy = remote(
                pieces.at[g, t],
                strips.at[me_n, g, here, :],
                a2a_send.at[g, t],
                a2a_recv.at[g, me_t],
                {"tile": t},
            )
            copy.start()
            a2a.append(copy)

    slabs = []

    def send_slab(owner, g, to, slot):
        copy = remote(
            strips.at[owner, g],
            strips.at[owner, g],
            slab_send.at[g, slot],
            slab_recv.at[g, owner],
            {"nest": to},
        )
        copy.start()
        slabs.append(copy)

    def wait_slab(owner, g):
        remote(
            strips.at[owner, g],
            strips.at[owner, g],
            slab_send.at[g, 0],
            slab_recv.at[g, owner],
            {"nest": owner},
        ).wait_recv()

    def flip(mask):
        if mask == 1:
            return me_n + 1 - 2 * lax.rem(me_n, 2)
        if mask == 2:
            return lax.rem(me_n + 2, 4)
        return 3 - me_n

    relayed = nests == 4

    def relay(g):
        first, second = (flip(1), flip(2)) if g % 2 == 0 else (flip(2), flip(1))
        wait_slab(first, g)
        send_slab(first, g, second, 2)

    for g in range(groups):
        for d in range(1, tiles):
            t = lax.rem(me_t + d, tiles)
            there = pl.ds(pl.multiple_of(t * prd, prd), prd)
            remote(
                pieces.at[g, t],
                strips.at[me_n, g, there, :],
                a2a_send.at[g, t],
                a2a_recv.at[g, t],
                {"tile": t},
            ).wait_recv()
        if relayed:
            send_slab(me_n, g, flip(1), 0)
            send_slab(me_n, g, flip(2), 1)
            if g:
                relay(g - 1)
        else:
            for d in range(1, nests):
                send_slab(me_n, g, lax.rem(me_n + d, nests), d - 1)
    if relayed:
        relay(groups - 1)

    own_start = me_n * rows
    place_r = lax.rem(lax.broadcasted_iota(jnp.int32, (2 * nrows, rows), 0), nrows)
    place_c = lax.broadcasted_iota(jnp.int32, (2 * nrows, rows), 1)
    prio = prio_ref[...]
    west_t, east_t = lax.rem(me_t + tiles - 1, tiles), lax.rem(me_t + 1, tiles)
    low_n, high_n = lax.rem(me_n + nests - 1, nests), lax.rem(me_n + 1, nests)
    lane = lax.broadcasted_iota(jnp.int32, (cols, LANES), 1)
    places = []
    for n in range(nests):
        hit = place_c - place_r == offs_ref[n, 0] - own_start
        places.append(jnp.where(hit, 1.0, 0.0).astype(BF16))

    edges = []
    parent_in.wait()
    for g in range(groups):
        if relayed:
            first, second = (flip(1), flip(2)) if g % 2 == 0 else (flip(2), flip(1))
            wait_slab(second, g)
            wait_slab(flip(3), g)
        else:
            for d in range(1, nests):
                wait_slab(lax.rem(me_n + d, nests), g)
        now = merged[g * per : (g + 1) * per]
        for n in range(nests):
            slab = jnp.concatenate(split(strips[n, g]), axis=0)
            placed = lax.dot_general(
                slab, places[n], (((0,), (0,)), ((), ())), preferred_element_type=F32
            )
            now = jnp.where((prio == n)[None], placed.reshape(per, cols, rows), now)
        merged[g * per : (g + 1) * per] = now
        low = jnp.zeros((cols, LANES), F32)
        high = jnp.zeros((cols, LANES), F32)
        for j in range(per):
            low = jnp.where(lane == j, now[j, :, :1], low)
            high = jnp.where(lane == j, now[j, :, rows - 1 :], high)
            ew_out[g, 0, j : j + 1] = now[j, :1]
            ew_out[g, 1, j : j + 1] = now[j, cols - 1 :]
        ns_out[g, 0] = low
        ns_out[g, 1] = high
        for side, (source, target, where) in enumerate(
            (
                (ew_out.at[g, 0], ew_in.at[g, 0], {"tile": west_t}),
                (ew_out.at[g, 1], ew_in.at[g, 1], {"tile": east_t}),
                (ns_out.at[g, 0], ns_in.at[g, 0], {"nest": low_n}),
                (ns_out.at[g, 1], ns_in.at[g, 1], {"nest": high_n}),
            )
        ):
            copy = remote(source, target, edge_send.at[g, side], edge_recv.at[g, side], where)
            copy.start()
            edges.append(copy)

    row_lane = lax.broadcasted_iota(jnp.int32, (cols, rows), 1)
    outs = []
    for g in range(groups):
        for side in range(4):
            edges[4 * g + side].wait_recv()
        for j in range(per):
            f = g * per + j
            now = merged[f]
            east = jnp.concatenate([now[1:], ew_in[g, 0, j : j + 1]], axis=0)
            west = jnp.concatenate([ew_in[g, 1, j : j + 1], now[:-1]], axis=0)
            above = jnp.where(me_n == nests - 1, now[:, rows - 1 :], ns_in[g, 0, :, j : j + 1])
            below = jnp.where(me_n == 0, now[:, :1], ns_in[g, 1, :, j : j + 1])
            north = jnp.where(row_lane == rows - 1, above, pltpu.roll(now, rows - 1, 1))
            south = jnp.where(row_lane == 0, below, pltpu.roll(now, 1, 1))
            result[f] = now + rate_ref[f] * (east + west + north + south - 4.0 * now)
        copy = pltpu.make_async_copy(group(result, g), group(out_hbm, g), out_sem.at[g])
        copy.start()
        outs.append(copy)

    for copy in a2a + slabs + edges:
        copy.wait_send()
    for copy in outs:
        copy.wait()


def per_device(
    child_fields, row_weights, col_weights, nest_offsets, priority, parent_old, smooth_rate
):
    planes, crow, ccols = child_fields.shape[1:]
    prd = row_weights.shape[0]
    _, cols, rows = parent_old.shape
    tiles, nests = lax.axis_size("tile"), lax.axis_size("nest")
    per = LANES // cols
    groups = planes // per
    nrows = prd * tiles
    smem = pl.BlockSpec(memory_space=pltpu.SMEM)
    vmem = pl.BlockSpec(memory_space=pltpu.VMEM)
    hbm = pl.BlockSpec(memory_space=pl.ANY)
    dma = pltpu.SemaphoreType.DMA
    return pl.pallas_call(
        functools.partial(kernel, tiles, nests),
        out_shape=jax.ShapeDtypeStruct(parent_old.shape, F32),
        in_specs=[smem, smem, vmem, vmem, hbm, hbm, hbm],
        out_specs=hbm,
        scratch_shapes=[
            pltpu.VMEM((planes, crow, ccols), F32),
            pltpu.VMEM(col_weights.shape, F32),
            pltpu.VMEM((planes, cols, rows), F32),
            pltpu.VMEM((groups, tiles, prd, LANES), F32),
            pltpu.VMEM((nests, groups, nrows, LANES), F32),
            pltpu.VMEM((groups, 2, per, rows), F32),
            pltpu.VMEM((groups, 2, per, rows), F32),
            pltpu.VMEM((groups, 2, cols, LANES), F32),
            pltpu.VMEM((groups, 2, cols, LANES), F32),
            pltpu.VMEM((planes, cols, rows), F32),
            dma((groups,)),
            dma,
            dma,
            dma((groups,)),
            dma((groups, tiles)),
            dma((groups, tiles)),
            dma((groups, max(nests - 1, 3))),
            dma((groups, nests)),
            dma((groups, 4)),
            dma((groups, 4)),
        ],
        compiler_params=pltpu.CompilerParams(
            collective_id=0, has_side_effects=True, vmem_limit_bytes=60 * 1024 * 1024
        ),
    )(nest_offsets, smooth_rate, row_weights, priority, child_fields, col_weights, parent_old)


def solution(mesh):
    return jax.shard_map(
        per_device,
        mesh=mesh,
        in_specs=(
            P("nest", None, "tile", None),
            P(),
            P(),
            P(),
            P("tile", "nest"),
            P(None, "tile", "nest"),
            P(),
        ),
        out_specs=P(None, "tile", "nest"),
        check_vma=False,
    )
```

time: 77 us -> 28.7 us (0.37)
  Pallas kernels: 0 us -> 25.2 us
  local copies, waits for them, and re-layouts: 26.5 us -> 3.2 us
  waiting for transfers between devices: 15.8 us -> 0 us
  blocking collectives: 12.9 us -> 0 us
  starting transfers between devices: 9.88 us -> 0 us
  between operations: 4.73 us -> 0.01 us
  other arithmetic: 4.38 us -> 0 us
  matrix products: 1.93 us -> 0 us
    pallas_call x0 -> x1, Pallas kernels: none -> 25.2 us  [per_device(): pl.pallas_call(functools.partial(kernel, tiles, nests), out_shape=jax.Sha...]
    dynamic_update_slice x4 -> x0, local copies, waits for them, and re-layouts: 20.9 us -> none  [place_slabs(): lax.dynamic_update_slice(framed, slabs[member], (jnp.int32(0), jnp.int32(...]
    all_gather x1 -> x0, blocking collectives: 12.9 us -> none  [per_device(): lax.all_gather(column_slab[None], 'nest', axis=0, tiled=True)]
    ppermute x4 -> x0, waiting for transfers between devices: 11.7 us -> none  [the longest x2 10.7 us: with_halo(): before = lax.ppermute(last, axis, up)]
    all_to_all x1 -> x0, starting transfers between devices: 6.35 us -> none  [per_device(): lax.all_to_all(outgoing, 'tile', split_axis=0, concat_axis=0, tiled=True)]
    all_to_all x1 -> x0, waiting for transfers between devices: 4.14 us -> none  [per_device(): lax.all_to_all(outgoing, 'tile', split_axis=0, concat_axis=0, tiled=True)]
    ppermute x4 -> x0, starting transfers between devices: 3.52 us -> none  [the longest x2 2.97 us: with_halo(): after = lax.ppermute(leading, axis, down)]
    unnamed x10 -> x2, local copies, waits for them, and re-layouts: 0.02 us -> 3.2 us
  transfers between devices with their start and end apart: 5 -> 0, of which waited for: 4 -> 0; matrix products, arithmetic and copies ran while one was open for 0% -> 0% of each run, Pallas kernels for 0% -> 0%
where the time goes in v1:
time: 28.7 us; the launch traced here: 28.5 us
  Pallas kernels  25.2 us (88%)
  local copies, waits for them, and re-layouts  3.2 us (11%)
    pallas_call x1, Pallas kernels, per_device(): pl.pallas_call(functools.partial(kernel, tiles, nests), out_shape=jax.Sha...  25.2 us
    unnamed x2, local copies, waits for them, and re-layouts  3.2 us

profile of v1, /device:TPU:0, one launch (start us, length us, event | category | flops | bytes accessed | tf_op | source)
XLA Modules:
  0.0 28.5 jit_solution(1787152729091467869)
XLA Ops:
  0.0 1.3 %copy.8.offs_ref = s32[4,2]{1,0:T(4,128)} copy(s32[4,2]{0,1:T(2,128)} %param.10) | data formatting | bytes 64 | tf_op args[3]
  1.3 25.2 %shard_map.73 = f32[32,16,256]{2,1,0:T(8,128)} custom-call(s32[4,2]{1,0:T(4,128)} %copy.8.offs_ref, f32[32]{0:T(128)} %rate_ref.1, f32[8,24]{1,0:T(8,128)} %rw_ref.1, s32[16,256]{1,0:T(8,128)} %prio_ref.1, f32[1,32,24,384]{3,2,1,0:T(8,128)} %child_hbm.1, f32[384,128]{1,0:T(8,128)} %cw_hbm.1, f32[32,16,256]{2,1,0:T(8,128)} %parent_hbm.1), custom_call_target="tpu_custom_call" | custom-call | tf_op jit(solution)/shard_map/pallas_call | solution.py:311
  26.6 1.9 %copy.10 = f32[32,16,256]{2,1,0:T(8,128)} copy(f32[32,16,256]{2,1,0:T(8,128)} %shard_map.73) | data formatting | bytes 1048576

commit v2 on v1

--- a/solution.py
+++ b/solution.py
@@ -121,17 +121,17 @@
     lane_group = lax.broadcasted_iota(jnp.int32, (prd, LANES), 1) // cols
     left = jnp.int32(0)
     for n in range(nests):
-        left = jnp.where(me_n == n, offs_ref[n, 1], left)
-
-    a2a = []
-    cw_split = None
-    for g in range(groups):
+        left = jnp.where(me_n == n, offs_ref[1, n], left)
+
+    a2a, cw_split = [], []
+
+    def restrict(g):
         child_in[g].wait()
         block = child[g * per : (g + 1) * per].reshape(per * crow, child.shape[2])
         thinned = dot3(block_rw, split(block))
-        if g == 0:
+        if not cw_split:
             cw_in.wait()
-            cw_split = split(cw[...])
+            cw_split.extend(split(cw[...]))
         restricted = dot3(split(thinned), cw_split)
         restricted = pltpu.roll(restricted, left, 1)
         for t in range(tiles):
@@ -192,11 +192,13 @@
     relayed = nests == 4
 
     def relay(g):
+        if not relayed:
+            return
         first, second = (flip(1), flip(2)) if g % 2 == 0 else (flip(2), flip(1))
         wait_slab(first, g)
         send_slab(first, g, second, 2)
 
-    for g in range(groups):
+    def forward(g):
         for d in range(1, tiles):
             t = lax.rem(me_t + d, tiles)
             there = pl.ds(pl.multiple_of(t * prd, prd), prd)
@@ -208,15 +210,11 @@
                 {"tile": t},
             ).wait_recv()
         if relayed:
-            send_slab(me_n, g, flip(1), 0)
-            send_slab(me_n, g, flip(2), 1)
-            if g:
-                relay(g - 1)
+            send_slab(me_n, g, flip(1 + g % 2), 0)
+            send_slab(me_n, g, flip(2 - g % 2), 1)
         else:
             for d in range(1, nests):
                 send_slab(me_n, g, lax.rem(me_n + d, nests), d - 1)
-    if relayed:
-        relay(groups - 1)
 
     own_start = me_n * rows
     place_r = lax.rem(lax.broadcasted_iota(jnp.int32, (2 * nrows, rows), 0), nrows)
@@ -227,12 +225,14 @@
     lane = lax.broadcasted_iota(jnp.int32, (cols, LANES), 1)
     places = []
     for n in range(nests):
-        hit = place_c - place_r == offs_ref[n, 0] - own_start
+        hit = place_c - place_r == offs_ref[0, n] - own_start
         places.append(jnp.where(hit, 1.0, 0.0).astype(BF16))
 
-    edges = []
-    parent_in.wait()
-    for g in range(groups):
+    edges = {}
+
+    def merge(g):
+        if g == 0:
+            parent_in.wait()
         if relayed:
             first, second = (flip(1), flip(2)) if g % 2 == 0 else (flip(2), flip(1))
             wait_slab(second, g)
@@ -267,13 +267,15 @@
         ):
             copy = remote(source, target, edge_send.at[g, side], edge_recv.at[g, side], where)
             copy.start()
-            edges.append(copy)
+            edges[g, side] = copy
 
     row_lane = lax.broadcasted_iota(jnp.int32, (cols, rows), 1)
     outs = []
-    for g in range(groups):
+
+    def finish(g):
         for side in range(4):
-            edges[4 * g + side].wait_recv()
+            edges[g, side].wait_recv()
+        smoothed = []
         for j in range(per):
             f = g * per + j
             now = merged[f]
@@ -283,12 +285,20 @@
             below = jnp.where(me_n == 0, now[:, :1], ns_in[g, 1, :, j : j + 1])
             north = jnp.where(row_lane == rows - 1, above, pltpu.roll(now, rows - 1, 1))
             south = jnp.where(row_lane == 0, below, pltpu.roll(now, 1, 1))
-            result[f] = now + rate_ref[f] * (east + west + north + south - 4.0 * now)
+            smoothed.append(now + rate_ref[f] * (east + west + north + south - 4.0 * now))
+        for j in range(per):
+            result[g * per + j] = smoothed[j]
         copy = pltpu.make_async_copy(group(result, g), group(out_hbm, g), out_sem.at[g])
         copy.start()
         outs.append(copy)
 
-    for copy in a2a + slabs + edges:
+    lags = ((restrict, 0), (forward, 1), (relay, 2), (merge, 3), (finish, 5))
+    for step in range(groups + 5):
+        for stage, lag in lags:
+            if 0 <= step - lag < groups:
+                stage(step - lag)
+
+    for copy in a2a + slabs + list(edges.values()):
         copy.wait_send()
     for copy in outs:
         copy.wait()
@@ -338,7 +348,7 @@
         compiler_params=pltpu.CompilerParams(
             collective_id=0, has_side_effects=True, vmem_limit_bytes=60 * 1024 * 1024
         ),
-    )(nest_offsets, smooth_rate, row_weights, priority, child_fields, col_weights, parent_old)
+    )(nest_offsets.T, smooth_rate, row_weights, priority, child_fields, col_weights, parent_old)
 
 
 def solution(mesh):

time: 28.7 us -> 31.3 us (1.091)
  Pallas kernels: 25.2 us -> 29.1 us
  local copies, waits for them, and re-layouts: 3.2 us -> 1.87 us
    pallas_call x1, Pallas kernels: 25.2 us -> 29.1 us  [per_device(): pl.pallas_call(functools.partial(kernel, tiles, nests), out_shape=jax.Sha...]
    unnamed x2 -> x1, local copies, waits for them, and re-layouts: 3.2 us -> 1.87 us
where the time goes in v2:
time: 31.3 us; the launch traced here: 31 us
  Pallas kernels  29.1 us (93%)
  local copies, waits for them, and re-layouts  1.87 us (6%)
    pallas_call x1, Pallas kernels, per_device(): pl.pallas_call(functools.partial(kernel, tiles, nests), out_shape=jax.Sha...  29.1 us
    unnamed x1, local copies, waits for them, and re-layouts  1.87 us

profile of v2, /device:TPU:0, one launch (start us, length us, event | category | flops | bytes accessed | tf_op | source)
XLA Modules:
  0.0 31.0 jit_solution(12847922396805226751)
XLA Ops:
  0.0 29.1 %shard_map.73 = f32[32,16,256]{2,1,0:T(8,128)} custom-call(s32[2,4]{1,0:T(2,128)} %bitcast.1, f32[32]{0:T(128)} %rate_ref.1, f32[8,24]{1,0:T(8,128)} %rw_ref.1, s32[16,256]{1,0:T(8,128)} %prio_ref.1, f32[1,32,24,384]{3,2,1,0:T(8,128)} %child_hbm.1, f32[384,128]{1,0:T(8,128)} %cw_hbm.1, f32[32,16,256]{2,1,0:T(8,128)} %parent_hbm.1), custom_call_target="tpu_custom_call" | custom-call | tf_op jit(solution)/shard_map/pallas_call | solution.py:321
  29.1 1.9 %copy.9 = f32[32,16,256]{2,1,0:T(8,128)} copy(f32[32,16,256]{2,1,0:T(8,128)} %shard_map.73) | data formatting | bytes 1048576

commit v3 on v2

--- a/solution.py
+++ b/solution.py
@@ -38,17 +38,32 @@
     )
 
 
+def order(groups):
+    yield "R", 0
+    for g in range(1, groups):
+        yield "R", g
+        if g == 1:
+            yield "S", 0
+        yield "S", g
+    if groups == 1:
+        yield "S", 0
+    for stage in "FME":
+        yield from ((stage, g) for g in range(groups))
+
+
 def kernel(
     tiles,
     nests,
     offs_ref,
     rate_ref,
-    rw_ref,
-    prio_ref,
+    rw_hbm,
+    prio_hbm,
     child_hbm,
     cw_hbm,
     parent_hbm,
     out_hbm,
+    rw_ref,
+    prio_ref,
     child,
     cw,
     merged,
@@ -59,6 +74,7 @@
     ns_out,
     ns_in,
     result,
+    small_sem,
     child_sem,
     cw_sem,
     parent_sem,
@@ -87,12 +103,6 @@
     ]
     cw_in = pltpu.make_async_copy(cw_hbm, cw, cw_sem)
     parent_in = pltpu.make_async_copy(parent_hbm, merged, parent_sem)
-    child_in[0].start()
-    cw_in.start()
-    for g in range(1, groups):
-        child_in[g].start()
-    parent_in.start()
-
     barrier = pltpu.get_barrier_semaphore()
     for d in range(1, tiles):
         pl.semaphore_signal(
@@ -102,7 +112,17 @@
         pl.semaphore_signal(
             barrier, inc=1, device_id={"nest": lax.rem(me_n + d, nests)}, device_id_type=MESH
         )
-
+    rw_in = pltpu.make_async_copy(rw_hbm, rw_ref, small_sem.at[0])
+    prio_in = pltpu.make_async_copy(prio_hbm, prio_ref, small_sem.at[1])
+    rw_in.start()
+    child_in[0].start()
+    cw_in.start()
+    for g in range(1, groups):
+        child_in[g].start()
+    prio_in.start()
+    parent_in.start()
+
+    rw_in.wait()
     rw = rw_ref[...]
     spread_rows = lax.broadcasted_iota(jnp.int32, (per * crow, crow), 0)
     spread_cols = lax.broadcasted_iota(jnp.int32, (per * crow, crow), 1)
@@ -124,6 +144,8 @@
         left = jnp.where(me_n == n, offs_ref[1, n], left)
 
     a2a, cw_split = [], []
+
+    here = pl.ds(pl.multiple_of(me_t * prd, prd), prd)
 
     def restrict(g):
         child_in[g].wait()
@@ -144,8 +166,9 @@
                     part = pltpu.roll(part, shift, 1)
                 piece = part if j == 0 else jnp.where(lane_group == j, part, piece)
             pieces[g, t] = piece
-        here = pl.ds(pl.multiple_of(me_t * prd, prd), prd)
         strips[me_n, g, here, :] = pieces[g, me_t]
+
+    def send(g):
         if g == 0:
             pl.semaphore_wait(barrier, tiles + nests - 2)
         for d in range(1, tiles):
@@ -182,22 +205,6 @@
             {"nest": owner},
         ).wait_recv()
 
-    def flip(mask):
-        if mask == 1:
-            return me_n + 1 - 2 * lax.rem(me_n, 2)
-        if mask == 2:
-            return lax.rem(me_n + 2, 4)
-        return 3 - me_n
-
-    relayed = nests == 4
-
-    def relay(g):
-        if not relayed:
-            return
-        first, second = (flip(1), flip(2)) if g % 2 == 0 else (flip(2), flip(1))
-        wait_slab(first, g)
-        send_slab(first, g, second, 2)
-
     def forward(g):
         for d in range(1, tiles):
             t = lax.rem(me_t + d, tiles)
@@ -209,16 +216,13 @@
                 a2a_recv.at[g, t],
                 {"tile": t},
             ).wait_recv()
-        if relayed:
-            send_slab(me_n, g, flip(1 + g % 2), 0)
-            send_slab(me_n, g, flip(2 - g % 2), 1)
-        else:
-            for d in range(1, nests):
-                send_slab(me_n, g, lax.rem(me_n + d, nests), d - 1)
+        for d in range(1, nests):
+            send_slab(me_n, g, lax.rem(me_n + d, nests), d - 1)
 
     own_start = me_n * rows
     place_r = lax.rem(lax.broadcasted_iota(jnp.int32, (2 * nrows, rows), 0), nrows)
     place_c = lax.broadcasted_iota(jnp.int32, (2 * nrows, rows), 1)
+    prio_in.wait()
     prio = prio_ref[...]
     west_t, east_t = lax.rem(me_t + tiles - 1, tiles), lax.rem(me_t + 1, tiles)
     low_n, high_n = lax.rem(me_n + nests - 1, nests), lax.rem(me_n + 1, nests)
@@ -233,13 +237,8 @@
     def merge(g):
         if g == 0:
             parent_in.wait()
-        if relayed:
-            first, second = (flip(1), flip(2)) if g % 2 == 0 else (flip(2), flip(1))
-            wait_slab(second, g)
-            wait_slab(flip(3), g)
-        else:
-            for d in range(1, nests):
-                wait_slab(lax.rem(me_n + d, nests), g)
+        for d in range(1, nests):
+            wait_slab(lax.rem(me_n + d, nests), g)
         now = merged[g * per : (g + 1) * per]
         for n in range(nests):
             slab = jnp.concatenate(split(strips[n, g]), axis=0)
@@ -292,11 +291,9 @@
         copy.start()
         outs.append(copy)
 
-    lags = ((restrict, 0), (forward, 1), (relay, 2), (merge, 3), (finish, 5))
-    for step in range(groups + 5):
-        for stage, lag in lags:
-            if 0 <= step - lag < groups:
-                stage(step - lag)
+    stages = {"R": restrict, "S": send, "F": forward, "M": merge, "E": finish}
+    for step in order(groups):
+        stages[step[0]](step[1])
 
     for copy in a2a + slabs + list(edges.values()):
         copy.wait_send()
@@ -315,15 +312,16 @@
     groups = planes // per
     nrows = prd * tiles
     smem = pl.BlockSpec(memory_space=pltpu.SMEM)
-    vmem = pl.BlockSpec(memory_space=pltpu.VMEM)
     hbm = pl.BlockSpec(memory_space=pl.ANY)
     dma = pltpu.SemaphoreType.DMA
     return pl.pallas_call(
         functools.partial(kernel, tiles, nests),
         out_shape=jax.ShapeDtypeStruct(parent_old.shape, F32),
-        in_specs=[smem, smem, vmem, vmem, hbm, hbm, hbm],
+        in_specs=[smem, smem] + [hbm] * 5,
         out_specs=hbm,
         scratch_shapes=[
+            pltpu.VMEM(row_weights.shape, F32),
+            pltpu.VMEM((cols, rows), jnp.int32),
             pltpu.VMEM((planes, crow, ccols), F32),
             pltpu.VMEM(col_weights.shape, F32),
             pltpu.VMEM((planes, cols, rows), F32),
@@ -334,19 +332,20 @@
             pltpu.VMEM((groups, 2, cols, LANES), F32),
             pltpu.VMEM((groups, 2, cols, LANES), F32),
             pltpu.VMEM((planes, cols, rows), F32),
+            dma((2,)),
             dma((groups,)),
             dma,
             dma,
             dma((groups,)),
             dma((groups, tiles)),
             dma((groups, tiles)),
-            dma((groups, max(nests - 1, 3))),
+            dma((groups, nests - 1)),
             dma((groups, nests)),
             dma((groups, 4)),
             dma((groups, 4)),
         ],
         compiler_params=pltpu.CompilerParams(
-            collective_id=0, has_side_effects=True, vmem_limit_bytes=60 * 1024 * 1024
+            collective_id=0, has_side_effects=True, vmem_limit_bytes=60 * 2**20
         ),
     )(nest_offsets.T, smooth_rate, row_weights, priority, child_fields, col_weights, parent_old)
 

time: 31.3 us -> 26.1 us (0.83)
  Pallas kernels: 29.1 us -> 24 us
    pallas_call x1, Pallas kernels: 29.1 us -> 24 us  [per_device(): pl.pallas_call(functools.partial(kernel, tiles, nests), out_shape=jax.Sha...]
where the time goes in v3:
time: 26.1 us; the launch traced here: 25.9 us
  Pallas kernels  24 us (92%)
  local copies, waits for them, and re-layouts  1.87 us (7%)
    pallas_call x1, Pallas kernels, per_device(): pl.pallas_call(functools.partial(kernel, tiles, nests), out_shape=jax.Sha...  24 us
    unnamed x1, local copies, waits for them, and re-layouts  1.87 us

profile of v3, /device:TPU:0, one launch (start us, length us, event | category | flops | bytes accessed | tf_op | source)
XLA Modules:
  0.0 25.9 jit_solution(4232105975153628313)
XLA Ops:
  0.0 24.0 %shard_map.73 = f32[32,16,256]{2,1,0:T(8,128)} custom-call(s32[2,4]{1,0:T(2,128)} %bitcast.1, f32[32]{0:T(128)} %rate_ref.1, f32[8,24]{1,0:T(8,128)} %rw_hbm.1, s32[16,256]{1,0:T(8,128)} %prio_hbm.1, f32[1,32,24,384]{3,2,1,0:T(8,128)} %child_hbm.1, f32[384,128]{1,0:T(8,128)} %cw_hbm.1, f32[32,16,256]{2,1,0:T(8,128)} %parent_hbm.1), custom_call_target="tpu_custom_call" | custom-call | tf_op jit(solution)/shard_map/pallas_call | solution.py:317
  24.0 1.9 %copy.9 = f32[32,16,256]{2,1,0:T(8,128)} copy(f32[32,16,256]{2,1,0:T(8,128)} %shard_map.73) | data formatting | bytes 1048576

commit v4 on v3

--- a/solution.py
+++ b/solution.py
@@ -61,7 +61,7 @@
     child_hbm,
     cw_hbm,
     parent_hbm,
-    out_hbm,
+    result,
     rw_ref,
     prio_ref,
     child,
@@ -73,12 +73,10 @@
     ew_in,
     ns_out,
     ns_in,
-    result,
     small_sem,
     child_sem,
     cw_sem,
     parent_sem,
-    out_sem,
     a2a_send,
     a2a_recv,
     slab_send,
@@ -269,8 +267,6 @@
             edges[g, side] = copy
 
     row_lane = lax.broadcasted_iota(jnp.int32, (cols, rows), 1)
-    outs = []
-
     def finish(g):
         for side in range(4):
             edges[g, side].wait_recv()
@@ -287,9 +283,6 @@
             smoothed.append(now + rate_ref[f] * (east + west + north + south - 4.0 * now))
         for j in range(per):
             result[g * per + j] = smoothed[j]
-        copy = pltpu.make_async_copy(group(result, g), group(out_hbm, g), out_sem.at[g])
-        copy.start()
-        outs.append(copy)
 
     stages = {"R": restrict, "S": send, "F": forward, "M": merge, "E": finish}
     for step in order(groups):
@@ -297,8 +290,6 @@
 
     for copy in a2a + slabs + list(edges.values()):
         copy.wait_send()
-    for copy in outs:
-        copy.wait()
 
 
 def per_device(
@@ -316,9 +307,9 @@
     dma = pltpu.SemaphoreType.DMA
     return pl.pallas_call(
         functools.partial(kernel, tiles, nests),
-        out_shape=jax.ShapeDtypeStruct(parent_old.shape, F32),
+        out_shape=pltpu.VMEM(parent_old.shape, F32),
         in_specs=[smem, smem] + [hbm] * 5,
-        out_specs=hbm,
+        out_specs=pl.BlockSpec(memory_space=pltpu.VMEM),
         scratch_shapes=[
             pltpu.VMEM(row_weights.shape, F32),
             pltpu.VMEM((cols, rows), jnp.int32),
@@ -331,12 +322,10 @@
             pltpu.VMEM((groups, 2, per, rows), F32),
             pltpu.VMEM((groups, 2, cols, LANES), F32),
             pltpu.VMEM((groups, 2, cols, LANES), F32),
-            pltpu.VMEM((planes, cols, rows), F32),
             dma((2,)),
             dma((groups,)),
             dma,
             dma,
-            dma((groups,)),
             dma((groups, tiles)),
             dma((groups, tiles)),
             dma((groups, nests - 1)),

time: 26.1 us -> 24.4 us (0.935)
  local copies, waits for them, and re-layouts: 1.87 us -> 0.8 us
  Pallas kernels: 24 us -> 23.4 us
    unnamed x1, local copies, waits for them, and re-layouts: 1.87 us -> 0.8 us
    pallas_call x1, Pallas kernels: 24 us -> 23.4 us  [per_device(): pl.pallas_call(functools.partial(kernel, tiles, nests), out_shape=pltpu.V...]
where the time goes in v4:
time: 24.4 us; the launch traced here: 24.2 us
  Pallas kernels  23.4 us (96%)
  local copies, waits for them, and re-layouts  0.8 us (3%)
    pallas_call x1, Pallas kernels, per_device(): pl.pallas_call(functools.partial(kernel, tiles, nests), out_shape=pltpu.V...  23.4 us
    unnamed x1, local copies, waits for them, and re-layouts  0.8 us

profile of v4, /device:TPU:0, one launch (start us, length us, event | category | flops | bytes accessed | tf_op | source)
XLA Modules:
  0.0 24.2 jit_solution(17742560570317392218)
XLA Ops:
  0.0 23.4 %shard_map.73 = f32[32,16,256]{2,1,0:T(8,128)S(1)} custom-call(s32[2,4]{1,0:T(2,128)} %bitcast.1, f32[32]{0:T(128)} %rate_ref.1, f32[8,24]{1,0:T(8,128)} %rw_hbm.1, s32[16,256]{1,0:T(8,128)} %prio_hbm.1, f32[1,32,24,384]{3,2,1,0:T(8,128)} %child_hbm.1, f32[384,128]{1,0:T(8,128)} %cw_hbm.1, f32[32,16,256]{2,1,0:T(8,128)} %parent_hbm.1), custom_call_target="tpu_custom_call" | custom-call | tf_op jit(solution)/shard_map/pallas_call | solution.py:308
  23.4 0.8 %copy.9 = f32[32,16,256]{2,1,0:T(8,128)} copy(f32[32,16,256]{2,1,0:T(8,128)S(1)} %shard_map.73) | data formatting | bytes 1048576
